TPU v7x, 16 devices: a 4x2x1 block of a 4x4x8 slice. The times are simulated.
16 devices in a mesh: dp: 2 (over y, z), dcp: 8 (over x, core).
Axes of the slice: x: 4, y: 2, z: 1, core: 2. Of those that a mesh axis runs over, the one named last changes fastest.
The devices are a block of a 4x4x8 slice.
Arguments:
- q_abs: bfloat16 [128, 128, 576], P('dp', 'dcp'), parts along dimension 0
- latent_cache: bfloat16 [128, 4, 8, 256, 576], P('dp', None, 'dcp'), parts along dimension 0
- ctx_len: int32 [128], P('dp'), parts along dimension 0
Outputs:
- output: bfloat16 [128, 128, 512], P(('dp', 'dcp')), parts along dimension 0
There are 2 independent parts. A program takes and returns all parts, laid end to end along the dimension named above; each array names one.
All inputs are finite; a program needn't handle non-finite values.
Results may differ from a plain program's by a relative error of at most 0.00644916.
Values are sent between devices in bfloat16 or wider.
A program may use at most 768 MiB of HBM per device.

v0:
```python
import jax
import jax.numpy as jnp
from jax import lax
from jax.sharding import PartitionSpec as P

ROPE_DIM = 64
QK_DIM = 192


def solution(mesh):
    group_size = mesh.shape['dcp']

    def local_step(q_blk, cache_blk, len_blk):
        batch_rows = q_blk.shape[0]
        num_pages = cache_blk.shape[1]
        page_len = cache_blk.shape[3]
        latent_dim = q_blk.shape[2] - ROPE_DIM
        out_rows = batch_rows // group_size
        dev_index = lax.axis_index('dcp')
        q_full = lax.all_gather(q_blk, 'dcp', axis=1, tiled=True)
        cache_own = cache_blk[:, :, 0]
        scores = jnp.einsum('bhw,bjtw->bhjt', q_full, cache_own, preferred_element_type=jnp.float32) * (QK_DIM ** -0.5)
        positions = (jnp.arange(num_pages)[:, None] * group_size + dev_index) * page_len + jnp.arange(page_len)[None, :]
        is_valid = positions[None] < len_blk[:, None, None]
        scores = jnp.where(is_valid[:, None], scores, -1e30)
        row_max = jnp.max(scores, axis=(2, 3))
        weights_exp = jnp.exp(scores - row_max[:, :, None, None])
        denom_sum = jnp.sum(weights_exp, axis=(2, 3))
        pv_sum = jnp.einsum('bhjt,bjtw->bhw', weights_exp.astype(jnp.bfloat16), cache_own, preferred_element_type=jnp.float32)
        part_out = (pv_sum[..., :latent_dim] / denom_sum[..., None]).astype(jnp.bfloat16)
        part_lse = row_max + jnp.log(denom_sum)
        recv_out = lax.all_to_all(part_out, 'dcp', 0, 0, tiled=True).reshape(group_size, out_rows, part_out.shape[1], latent_dim)
        recv_lse = lax.all_to_all(part_lse, 'dcp', 0, 0, tiled=True).reshape(group_size, out_rows, part_lse.shape[1])
        total_lse = jax.nn.logsumexp(recv_lse, axis=0)
        merge_weights = jnp.exp(recv_lse - total_lse[None])
        merged = jnp.sum(merge_weights[..., None] * recv_out.astype(jnp.float32), axis=0)
        return merged.astype(jnp.bfloat16)

    return jax.shard_map(local_step, mesh=mesh, in_specs=(P('dp', 'dcp', None), P('dp', None, 'dcp', None, None), P('dp')), out_specs=P(('dp', 'dcp'), None, None), check_vma=False)
```

profile of v0, /device:TPU:112, one launch (start us, length us, event | category | flops | bytes accessed | tf_op | source)
XLA Modules:
  0.0 294.1 jit_solution(6148007578301479755)
XLA Ops:
  6.5 0.0 all-gather.2.cloned.1.call-start
  6.6 0.7 all-gather.2.cloned.1.call-update
  7.3 0.1 iota_add_fusion
  7.4 0.8 broadcast_compare_fusion
  8.2 58.0 %all-gather.2.cloned.1.call-done = bf16[64,128,576]{2,1,0:T(8,128)(2,1)} async-done(((bf16[64,16,576]{2,1,0:T(8,128)(2,1)}), bf16[64,128,576]{2,1,0:T(8,128)(2,1)}) %all-gather.2.cloned.1.call-update) | async-done | bytes 9437200 | tf_op jit(solution)/shard_map/all_gather | solution.py:20
  66.2 41.4 %fusion.4 = (f32[64,128]{1,0:T(8,128)S(1)}, f32[64,128,4,256]{3,1,2,0:T(8,128)}) fusion(pred[64,4,256]{2,1,0:T(4,128)(4,1)S(1)} %broadcast_compare_fusion, bf16[64,4,1,256,576]{3,4,2,1,0:T(8,128)(2,1)} %param.4, bf16[64,128,576]{2,1,0:T(8,128)(2,1)} %all-gather.2.cloned.1.call-done), kind=kOutput, calls=%fused_computation.6 | convolution fusion | flops 9688834048 | bytes 118587392 | tf_op jit(solution)/shard_map/bhw,bjtw->bhjt/dot_general | solution.py:22
  107.6 15.0 %fusion.6 = f32[64,128]{1,0:T(8,128)S(1)} fusion(f32[64,128,4,256]{3,1,2,0:T(8,128)} %get-tuple-element.6, f32[64,128]{1,0:T(8,128)S(1)} %get-tuple-element.5, pred[64,4,256]{2,1,0:T(4,128)(4,1)S(1)} %broadcast_compare_fusion), kind=kLoop, calls=%fused_computation.8 | loop fusion | flops 33546240 | bytes 33685504 | tf_op jit(solution)/shard_map/reduce_sum | solution.py:28
  122.6 45.5 %fusion.15 = f32[64,128,576]{2,1,0:T(8,128)} fusion(bf16[64,4,1,256,576]{3,4,2,1,0:T(8,128)(2,1)} %param.4, f32[64,128,4,256]{3,1,2,0:T(8,128)} %get-tuple-element.6, f32[64,128]{1,0:T(8,128)S(1)} %get-tuple-element.5, pred[64,4,256]{2,1,0:T(4,128)(4,1)S(1)} %broadcast_compare_fusion), kind=kOutput, calls=%fused_computation.18 | convolution fusion | flops 9697230848 | bytes 128024576 | tf_op jit(solution)/shard_map/bhjt,bjtw->bhw/dot_general | solution.py:29
  168.2 0.6 add_bitcast_fusion
  168.8 3.5 %all-to-all-start = ((f32[8,8,128]{2,1,0:T(8,128)}), f32[8,8,128]{2,1,0:T(8,128)S(1)}, u32[]{:S(2)}, u32[]{:S(2)}) async-start(f32[8,8,128]{2,1,0:T(8,128)} %add_bitcast_fusion), calls=%async_computation | async-start | bytes 65536 | tf_op jit(solution)/shard_map/all_to_all | solution.py:33
  172.3 9.2 %fusion.8 = bf16[64,128,512]{2,1,0:T(8,128)(2,1)} fusion(f32[64,128,576]{2,1,0:T(8,128)} %fusion.15, f32[64,128]{1,0:T(8,128)S(1)} %fusion.6), kind=kLoop, calls=%fused_computation.10 | loop fusion | flops 8388608 | bytes 25198592 | tf_op jit(solution)/shard_map/convert_element_type | solution.py:30
  181.5 0.0 all-to-all-done
  181.5 5.2 %all-to-all-start.1 = ((bf16[64,128,512]{2,1,0:T(8,128)(2,1)}), bf16[64,128,512]{2,1,0:T(8,128)(2,1)}, u32[]{:S(2)}, u32[]{:S(2)}) async-start(bf16[64,128,512]{2,1,0:T(8,128)(2,1)} %fusion.8), calls=%async_computation.1 | async-start | bytes 16777216 | tf_op jit(solution)/shard_map/all_to_all | solution.py:32
  186.9 94.3 %all-to-all-done.1 = bf16[64,128,512]{2,1,0:T(8,128)(2,1)} async-done(((bf16[64,128,512]{2,1,0:T(8,128)(2,1)}), bf16[64,128,512]{2,1,0:T(8,128)(2,1)}, u32[]{:S(2)}, u32[]{:S(2)}) %all-to-all-start.1) | async-done | bytes 8388640 | tf_op jit(solution)/shard_map/all_to_all | solution.py:32
  281.1 6.1 %fusion.9 = bf16[8,128,512]{2,1,0:T(8,128)(2,1)} fusion(bf16[8,8,128,512]{3,2,1,0:T(8,128)(2,1)} %bitcast.8, f32[8,8,128]{2,1,0:T(8,128)S(1)} %subtract_exponential_fusion.1), kind=kLoop, calls=%fused_computation.12 | loop fusion | flops 12058624 | bytes 9469952 | tf_op jit(solution)/shard_map/reduce_sum | solution.py:36
  (6 shorter events, 0.1 us)
Async XLA Ops:
  6.5 59.6 %all-gather.2.cloned.1.call-start = ((), (), s32[]{:S(2)}) async-start(), calls=%async_computation.2 | async-start | bytes 11796480 | tf_op jit(solution)/shard_map/all_gather | solution.py:20
  168.8 12.8 %all-to-all-start = ((f32[8,8,128]{2,1,0:T(8,128)}), f32[8,8,128]{2,1,0:T(8,128)S(1)}, u32[]{:S(2)}, u32[]{:S(2)}) async-start(f32[8,8,128]{2,1,0:T(8,128)} %add_bitcast_fusion), calls=%async_computation | async-start | bytes 65536 | tf_op jit(solution)/shard_map/all_to_all | solution.py:33
  181.5 99.6 %all-to-all-start.1 = ((bf16[64,128,512]{2,1,0:T(8,128)(2,1)}), bf16[64,128,512]{2,1,0:T(8,128)(2,1)}, u32[]{:S(2)}, u32[]{:S(2)}) async-start(bf16[64,128,512]{2,1,0:T(8,128)(2,1)} %fusion.8), calls=%async_computation.1 | async-start | bytes 16777216 | tf_op jit(solution)/shard_map/all_to_all | solution.py:32
Sparse Core Ops, SparseCore 0:
  8.9 57.1 all-gather.1
where the time goes:
time: 295 us; the launch traced here: 294 us
  waiting for transfers between devices  153 us (52%)
  matrix products  86.9 us (29%)
  other arithmetic  31.9 us (11%)
  between operations  13.5 us (5%)
  starting transfers between devices  8.77 us (3%)
    all_to_all x1, waiting for transfers between devices, local_step(): lax.all_to_all(part_out, 'dcp', 0, 0, tiled=True)  94.3 us
    all_gather x1, waiting for transfers between devices, local_step(): q_full = lax.all_gather(q_blk, 'dcp', axis=1, tiled=True)  58 us
    dot_general x1, matrix products, local_step(): jnp.einsum('bhjt,bjtw->bhw', weights_exp.astype(jnp.bfloat16), cache_own,...  45.5 us
    dot_general x1, matrix products, local_step(): jnp.einsum('bhw,bjtw->bhjt', q_full, cache_own, preferred_element_type=jn...  41.4 us
    reduce_sum x1, other arithmetic, local_step(): denom_sum = jnp.sum(weights_exp, axis=(2, 3))  15 us
    convert_element_type x1, other arithmetic, local_step(): (pv_sum[..., :latent_dim] / denom_sum[..., None]).astype(jnp.bfloat16)  9.19 us
    reduce_sum x1, other arithmetic, local_step(): jnp.sum(merge_weights[..., None] * recv_out.astype(jnp.float32), axis=0)  6.14 us
  transfers between devices with their start and end apart: 3, of which 2 were waited for; matrix products, arithmetic and copies ran while one was open for 3% of the time, Pallas kernels for 0%

commit v1 on v0

v1 whole, which is shorter than its diff:
```python
import functools

import jax
import jax.numpy as jnp
from jax import lax
from jax.experimental import pallas as pl
from jax.experimental.pallas import tpu as pltpu
from jax.sharding import PartitionSpec as P

ROPE_DIM = 64
QK_DIM = 192
CORES = 2
SLOTS = 4
AHEAD = 3
F32 = jnp.float32


def columns(row):
    return jnp.transpose(jnp.broadcast_to(row, (row.shape[1], row.shape[1])))


def weights(*lses):
    top = functools.reduce(jnp.maximum, lses)
    exps = [jnp.exp(one - top) for one in lses]
    total = functools.reduce(jnp.add, exps)
    return [columns(one / total) for one in exps], top + jnp.log(total)


def scaled(col, block):
    width = col.shape[1]
    return jnp.concatenate(
        [col * block[:, i : i + width] for i in range(0, block.shape[1], width)], axis=1
    )


def kernel(
    group, len_ref, q_hbm, c_hbm, out_hbm,
    qbuf, cbuf, osend, lsend, orecv, lrecv, own, lown, part, lpart, frecv, flrecv, drecv, dlrecv, outbuf,
    csem, qsem, ag_send, ag_recv, sib_send, sib_recv, ring_send, ring_recv, out_sem,
):
    rounds = qbuf.shape[0]
    chips = group // CORES
    steps = rounds * chips
    seqs = steps * CORES
    latent = osend.shape[2]
    half = latent // 2
    pages, width, page_len = cbuf.shape[1:]
    me = lax.axis_index('dcp')
    chip, core = me // CORES, me % CORES
    sibling = chip * CORES + 1 - core
    right = ((chip + 1) % chips) * CORES + core
    left = ((chip + chips - 1) % chips) * CORES + core
    far = ((chip + 2) % chips) * CORES + core

    def remote(src, dst, send, recv, target):
        return pltpu.make_async_remote_copy(
            src_ref=src, dst_ref=dst, send_sem=send, recv_sem=recv,
            device_id={'dcp': target}, device_id_type=pl.DeviceIdType.MESH)

    def place(n, other):
        r, k = n // chips, n % chips
        dest_chip = (chip + 2 - k + chips) % chips
        dest_core = (1 - core) if other else core
        return r, dest_chip * CORES + dest_core

    def fetch(n, e):
        r, d = place(n, e == 0)
        slot = (2 * n + e) % SLOTS
        return pltpu.make_async_copy(c_hbm.at[d, r, :, 0], cbuf.at[slot], csem.at[slot])

    def q_own(r):
        return pltpu.make_async_copy(q_hbm.at[:, r], qbuf.at[r, me], qsem.at[r])

    def q_copy(r, kind, block, target):
        return remote(qbuf.at[r, block], qbuf.at[r, block], ag_send.at[r, kind], ag_recv.at[r, kind], target)

    def q_first(r):
        q_copy(r, 0, me, right).start()
        q_copy(r, 1, me, left).start()
        q_copy(r, 3, me, sibling).start()

    def q_second(r):
        q_copy(r, 0, left, right).wait_recv()
        q_copy(r, 1, right, left).wait_recv()

        @pl.when(r % 2 == 0)
        def _():
            q_copy(r, 2, left, right).start()

        @pl.when(r % 2 == 1)
        def _():
            q_copy(r, 2, right, left).start()

        q_copy(r, 4, left, sibling).start()
        q_copy(r, 5, right, sibling).start()

    def q_third(r):
        q_copy(r, 2, far, right).wait_recv()
        q_copy(r, 6, far, sibling).start()

    def q_last(r):
        for kind in range(3, 7):
            q_copy(r, kind, me, sibling).wait_recv()

    def attend(n, e):
        r, d = place(n, e == 0)
        slot = (2 * n + e) % SLOTS
        fetch(n, e).wait()
        nxt = 2 * n + e + SLOTS - 1

        @pl.when(nxt < seqs)
        def _():
            fetch((2 * n + e + SLOTS - 1) // 2, (e + SLOTS - 1) % 2).start()

        heads = qbuf.shape[1] * qbuf.shape[3]
        q = qbuf[r, :, d].reshape(heads, width)
        length = len_ref[d * rounds + r]
        scores = []
        for j in range(pages):
            s = jnp.dot(q, cbuf[slot, j], preferred_element_type=F32) * (QK_DIM ** -0.5)
            pos = lax.broadcasted_iota(jnp.int32, s.shape, 1) + (j * group + me) * page_len
            scores.append(jnp.where(pos < length, s, -1e30))
        top = functools.reduce(jnp.maximum, [jnp.max(s, axis=1, keepdims=True) for s in scores])
        exps = [jnp.exp(s - top) for s in scores]
        total = functools.reduce(jnp.add, [jnp.sum(w, axis=1, keepdims=True) for w in exps])
        acc = functools.reduce(jnp.add, [
            lax.dot_general(w.astype(jnp.bfloat16), cbuf[slot, j, :latent], (((1,), (1,)), ((), ())),
                            preferred_element_type=F32)
            for j, w in enumerate(exps)])
        lse = top + jnp.log(total)
        lse = jnp.transpose(jnp.broadcast_to(lse, (heads, heads)))[0:1]
        return (acc / total).astype(jnp.bfloat16), lse

    def sib_o(n):
        return remote(osend.at[n], orecv.at[n], sib_send.at[n, 0], sib_recv.at[n, 0], sibling)

    def sib_l(n):
        return remote(lsend.at[n], lrecv.at[n], sib_send.at[n, 1], sib_recv.at[n, 1], sibling)

    def ring(r, kind):
        target = right if kind % 2 == 0 else left
        k = (0, 0, 1, 3, 1, 3)[kind]
        h = (0, 1, 1, 0, 0, 1)[kind]
        if kind < 2:
            dst, ldst = frecv.at[r, h], flrecv.at[r, h]
        else:
            side = kind % 2
            dst, ldst = drecv.at[r, side, h], dlrecv.at[r, side, h]
        return (
            remote(part.at[r, k, h], dst, ring_send.at[r, kind, 0], ring_recv.at[r, kind, 0], target),
            remote(lpart.at[r, k, h], ldst, ring_send.at[r, kind, 1], ring_recv.at[r, kind, 1], target),
        )

    def ring_start(r, kind):
        for copy in ring(r, kind):
            copy.start()

    def merge(n):
        r, k = n // chips, n % chips
        sib_o(n).wait_recv()
        sib_l(n).wait_recv()
        slot = n % 2
        (wa, wb), lse = weights(lown[slot], lrecv[n])
        for h in range(2):
            cols = pl.ds(h * half, half)
            part[r, k, h] = scaled(wa, own[slot, :, cols].astype(F32)) + scaled(wb, orecv[n, :, cols].astype(F32))
            lpart[r, k, h] = lse

        @pl.when(k == 0)
        def _():
            ring_start(r, 0)
            ring_start(r, 1)

        @pl.when(k == 1)
        def _():
            ring_start(r, 2)

        @pl.when(k == 3)
        def _():
            ring_start(r, 3)

    def relay(r):
        for kind in (4, 5):
            h = kind % 2
            k = (1, 3)[h]
            for copy in ring(r, h):
                copy.wait_recv()
            (wa, wb), lse = weights(lpart[r, k, h], flrecv[r, h])
            part[r, k, h] = scaled(wa, part[r, k, h]) + scaled(wb, frecv[r, h])
            lpart[r, k, h] = lse
            ring_start(r, kind)

    def out_copy(r):
        return pltpu.make_async_copy(outbuf.at[r], out_hbm.at[r], out_sem.at[r])

    def finish(r):
        for kind in (2, 3, 4, 5):
            for copy in ring(r, kind):
                copy.wait_recv()
        for h in range(2):
            (wa, wb, wc), _ = weights(lpart[r, 2, h], dlrecv[r, 0, h], dlrecv[r, 1, h])
            outbuf[r, :, pl.ds(h * half, half)] = (
                scaled(wa, part[r, 2, h]) + scaled(wb, drecv[r, 0, h]) + scaled(wc, drecv[r, 1, h])
            ).astype(jnp.bfloat16)
        out_copy(r).start()

    for r in range(rounds):
        q_own(r).start()
    for u in range(SLOTS - 1):
        fetch(u // 2, u % 2).start()
    barrier = pltpu.get_barrier_semaphore()
    for neighbour in (left, right, sibling):
        pl.semaphore_signal(barrier, inc=1, device_id={'dcp': neighbour}, device_id_type=pl.DeviceIdType.MESH)
    pl.semaphore_wait(barrier, 3)
    for r in range(rounds):
        q_own(r).wait()
    for r in range(AHEAD):
        q_first(r)
    q_second(0)
    q_first(AHEAD)
    q_second(1)
    q_first(AHEAD + 1)
    q_third(0)

    @pl.loop(0, rounds)
    def _(r):
        @pl.when(r + 2 < rounds)
        def _():
            q_second(r + 2)

        @pl.when(r + AHEAD + 2 < rounds)
        def _():
            q_first(r + AHEAD + 2)

        @pl.when(r + 1 < rounds)
        def _():
            q_third(r + 1)

        q_last(r)

        @pl.loop(0, chips)
        def _(k):
            n = r * chips + k
            o, lse = attend(n, 0)
            osend[n] = o
            lsend[n] = lse
            sib_o(n).start()
            sib_l(n).start()
            o, lse = attend(n, 1)
            own[n % 2] = o
            lown[n % 2] = lse

            @pl.when(n >= 1)
            def _():
                merge(n - 1)

        @pl.when(r >= 1)
        def _():
            relay(r - 1)

    merge(steps - 1)
    relay(rounds - 1)

    @pl.loop(0, rounds)
    def _(r):
        finish(r)

    @pl.loop(0, rounds)
    def _(r):
        out_copy(r).wait()
        for kind in range(6):
            for copy in ring(r, kind):
                copy.wait_send()
        q_copy(r, 0, me, right).wait_send()
        q_copy(r, 1, me, left).wait_send()
        for kind in range(2, 7):
            q_copy(r, kind, me, sibling).wait_send()

    @pl.loop(0, steps)
    def _(n):
        sib_o(n).wait_send()
        sib_l(n).wait_send()


def solution(mesh):
    group = mesh.shape['dcp']
    chips = group // CORES

    def local_step(q_blk, cache_blk, len_blk):
        batch, own_heads, width = q_blk.shape
        pages, page_len = cache_blk.shape[1], cache_blk.shape[3]
        latent = width - ROPE_DIM
        half = latent // 2
        rounds = batch // group
        heads = own_heads * group
        steps = rounds * chips
        q = q_blk.reshape(group, rounds, own_heads, width)
        cache = jnp.swapaxes(cache_blk, 3, 4).reshape(group, rounds, pages, 1, width, page_len)
        bf16 = jnp.bfloat16
        dma = pltpu.SemaphoreType.DMA
        return pl.pallas_call(
            functools.partial(kernel, group),
            out_shape=jax.ShapeDtypeStruct((rounds, heads, latent), bf16),
            in_specs=[
                pl.BlockSpec(memory_space=pltpu.SMEM),
                pl.BlockSpec(memory_space=pl.ANY),
                pl.BlockSpec(memory_space=pl.ANY),
            ],
            out_specs=pl.BlockSpec(memory_space=pl.ANY),
            scratch_shapes=[
                pltpu.VMEM((rounds, group, group, own_heads, width), bf16),
                pltpu.VMEM((SLOTS, pages, width, page_len), bf16),
                pltpu.VMEM((steps, heads, latent), bf16),
                pltpu.VMEM((steps, 1, heads), F32),
                pltpu.VMEM((steps, heads, latent), bf16),
                pltpu.VMEM((steps, 1, heads), F32),
                pltpu.VMEM((2, heads, latent), bf16),
                pltpu.VMEM((2, 1, heads), F32),
                pltpu.VMEM((rounds, chips, 2, heads, half), F32),
                pltpu.VMEM((rounds, chips, 2, 1, heads), F32),
                pltpu.VMEM((rounds, 2, heads, half), F32),
                pltpu.VMEM((rounds, 2, 1, heads), F32),
                pltpu.VMEM((rounds, 2, 2, heads, half), F32),
                pltpu.VMEM((rounds, 2, 2, 1, heads), F32),
                pltpu.VMEM((rounds, heads, latent), bf16),
                dma((SLOTS,)),
                dma((rounds,)),
                dma((rounds, 7)),
                dma((rounds, 7)),
                dma((steps, 2)),
                dma((steps, 2)),
                dma((rounds, 6, 2)),
                dma((rounds, 6, 2)),
                dma((rounds,)),
            ],
            compiler_params=pltpu.CompilerParams(
                collective_id=0, has_side_effects=True, vmem_limit_bytes=60000 * 1024),
        )(len_blk, q, cache)

    return jax.shard_map(
        local_step, mesh=mesh,
        in_specs=(P('dp', 'dcp', None), P('dp', None, 'dcp', None, None), P('dp')),
        out_specs=P(('dp', 'dcp'), None, None), check_vma=False)
```

time: 295 us -> 125 us (0.42)
  waiting for transfers between devices: 153 us -> 0 us
  Pallas kernels: 0 us -> 123 us
  matrix products: 86.9 us -> 0 us
  other arithmetic: 31.9 us -> 0 us
  between operations: 13.5 us -> 0.01 us
  starting transfers between devices: 8.77 us -> 0 us
    pallas_call x0 -> x1, Pallas kernels: none -> 123 us  [local_step(): pl.pallas_call(functools.partial(kernel, group), out_shape=jax.ShapeDtype...]
    all_to_all x2 -> x0, waiting for transfers between devices: 94.3 us -> none  [the longest x1 94.3 us: local_step(): lax.all_to_all(part_out, 'dcp', 0, 0, tiled=True)]
    dot_general x2 -> x0, matrix products: 86.9 us -> none  [the longest x1 45.5 us: local_step(): jnp.einsum('bhjt,bjtw->bhw', weights_exp.astype(jnp.bfloat16), cache_own,...]
    all_gather x1 -> x0, waiting for transfers between devices: 58 us -> none  [local_step(): q_full = lax.all_gather(q_blk, 'dcp', axis=1, tiled=True)]
    reduce_sum x3 -> x0, other arithmetic: 21.2 us -> none  [the longest x1 15 us: local_step(): denom_sum = jnp.sum(weights_exp, axis=(2, 3))]
    convert_element_type x1 -> x0, other arithmetic: 9.19 us -> none  [local_step(): (pv_sum[..., :latent_dim] / denom_sum[..., None]).astype(jnp.bfloat16)]
    all_to_all x2 -> x0, starting transfers between devices: 8.77 us -> none  [the longest x1 5.22 us: local_step(): lax.all_to_all(part_out, 'dcp', 0, 0, tiled=True)]
  transfers between devices with their start and end apart: 3 -> 0, of which waited for: 2 -> 0; matrix products, arithmetic and copies ran while one was open for 3% -> 0% of each run, Pallas kernels for 0% -> 0%
where the time goes in v1:
time: 125 us
  Pallas kernels  123 us (98%)
  local copies, waits for them, and re-layouts  2.26 us (2%)
    pallas_call x1, Pallas kernels, local_step(): pl.pallas_call(functools.partial(kernel, group), out_shape=jax.ShapeDtype...  123 us

profile of v1, /device:TPU:112, one launch (start us, length us, event | category | flops | bytes accessed | tf_op | source)
XLA Modules:
  0.0 125.1 jit_solution(3692599870459426921)
XLA Ops:
  0.0 122.8 %shard_map.37 = bf16[8,128,512]{2,1,0:T(8,128)(2,1)} custom-call(s32[64]{0:T(128)} %len_ref.1, bf16[8,8,16,576]{3,2,1,0:T(8,128)(2,1)} %bitcast.4, bf16[8,8,4,1,576,256]{5,4,3,2,1,0:T(8,128)(2,1)} %bitcast.2.c_hbm), custom_call_target="tpu_custom_call" | custom-call | tf_op jit(solution)/shard_map/pallas_call | solution.py:301
  122.8 2.3 %copy.5 = bf16[8,128,512]{2,1,0:T(8,128)(2,1)} copy(bf16[8,128,512]{2,1,0:T(8,128)(2,1)} %shard_map.37) | data formatting | bytes 2097152

commit v2 on v1

--- a/solution.py
+++ b/solution.py
@@ -12,6 +12,8 @@
 CORES = 2
 SLOTS = 4
 AHEAD = 3
+LANES = 128
+VMEM_BYTES = 46 * 2**20
 F32 = jnp.float32
 
 
@@ -34,11 +36,11 @@
 
 
 def kernel(
-    group, len_ref, q_hbm, c_hbm, out_hbm,
-    qbuf, cbuf, osend, lsend, orecv, lrecv, own, lown, part, lpart, frecv, flrecv, drecv, dlrecv, outbuf,
-    csem, qsem, ag_send, ag_recv, sib_send, sib_recv, ring_send, ring_recv, out_sem,
+    group, len_hbm, q_hbm, c_hbm, out_ref,
+    len_ref, rope, qbuf, cbuf, osend, lsend, orecv, lrecv, own, lown, part, lpart, frecv, flrecv, drecv, dlrecv,
+    lensem, csem, qsem, ag_send, ag_recv, sib_send, sib_recv, ring_send, f_recv, d_recv,
 ):
-    rounds = qbuf.shape[0]
+    rounds, _, tiles, own_heads, lanes = qbuf.shape
     chips = group // CORES
     steps = rounds * chips
     seqs = steps * CORES
@@ -68,39 +70,55 @@
         slot = (2 * n + e) % SLOTS
         return pltpu.make_async_copy(c_hbm.at[d, r, :, 0], cbuf.at[slot], csem.at[slot])
 
-    def q_own(r):
-        return pltpu.make_async_copy(q_hbm.at[:, r], qbuf.at[r, me], qsem.at[r])
+    latent_tiles = group * latent // lanes
+
+    def q_load():
+        yield pltpu.make_async_copy(q_hbm.at[:, :, :, latent:], rope, qsem.at[1])
+        for c in range(latent // lanes):
+            for r in range(rounds):
+                yield pltpu.make_async_copy(
+                    q_hbm.at[:, r, :, c * lanes : (c + 1) * lanes], qbuf.at[r, me, c * group : (c + 1) * group], qsem.at[0])
+
+    def q_pack():
+        pltpu.make_async_copy(rope, rope, qsem.at[1]).wait()
+        for r in range(rounds):
+            for p in range(group // 2):
+                qbuf[r, me, latent_tiles + p] = jnp.concatenate([rope[2 * p, r], rope[2 * p + 1, r]], axis=1)
+        whole = qbuf.at[:, me, 0:latent_tiles]
+        pltpu.make_async_copy(whole, whole, qsem.at[0]).wait()
 
     def q_copy(r, kind, block, target):
-        return remote(qbuf.at[r, block], qbuf.at[r, block], ag_send.at[r, kind], ag_recv.at[r, kind], target)
+        return remote(qbuf.at[r, block], qbuf.at[r, block], ag_send.at[0], ag_recv.at[r, kind], target)
+
+    def q_wait(r, kind, blocks):
+        ref = qbuf.at[r, 0:blocks]
+        pltpu.make_async_copy(ref, ref, ag_recv.at[r, kind]).wait()
 
     def q_first(r):
         q_copy(r, 0, me, right).start()
-        q_copy(r, 1, me, left).start()
-        q_copy(r, 3, me, sibling).start()
+        q_copy(r, 0, me, left).start()
+        q_copy(r, 2, me, sibling).start()
 
     def q_second(r):
-        q_copy(r, 0, left, right).wait_recv()
-        q_copy(r, 1, right, left).wait_recv()
+        q_wait(r, 0, 2)
 
         @pl.when(r % 2 == 0)
         def _():
-            q_copy(r, 2, left, right).start()
+            q_copy(r, 1, left, right).start()
 
         @pl.when(r % 2 == 1)
         def _():
-            q_copy(r, 2, right, left).start()
-
-        q_copy(r, 4, left, sibling).start()
-        q_copy(r, 5, right, sibling).start()
+            q_copy(r, 1, right, left).start()
+
+        q_copy(r, 2, left, sibling).start()
+        q_copy(r, 2, right, sibling).start()
 
     def q_third(r):
-        q_copy(r, 2, far, right).wait_recv()
-        q_copy(r, 6, far, sibling).start()
+        q_wait(r, 1, 1)
+        q_copy(r, 2, far, sibling).start()
 
     def q_last(r):
-        for kind in range(3, 7):
-            q_copy(r, kind, me, sibling).wait_recv()
+        q_wait(r, 2, chips)
 
     def attend(n, e):
         r, d = place(n, e == 0)
@@ -112,8 +130,11 @@
         def _():
             fetch((2 * n + e + SLOTS - 1) // 2, (e + SLOTS - 1) % 2).start()
 
-        heads = qbuf.shape[1] * qbuf.shape[3]
-        q = qbuf[r, :, d].reshape(heads, width)
+        heads = group * own_heads
+        q = [qbuf[r, :, c * group + d].reshape(heads, lanes) for c in range(latent // lanes)]
+        pair = qbuf[r, :, latent_tiles + d // 2].reshape(heads, lanes)
+        q.append(jnp.where(d % 2 == 0, pair[:, : lanes // 2], pair[:, lanes // 2 :]))
+        q = jnp.concatenate(q, axis=1)
         length = len_ref[d * rounds + r]
         scores = []
         for j in range(pages):
@@ -132,23 +153,23 @@
         return (acc / total).astype(jnp.bfloat16), lse
 
     def sib_o(n):
-        return remote(osend.at[n], orecv.at[n], sib_send.at[n, 0], sib_recv.at[n, 0], sibling)
+        return remote(osend.at[n], orecv.at[n], sib_send.at[0], sib_recv.at[n % 4, 0], sibling)
 
     def sib_l(n):
-        return remote(lsend.at[n], lrecv.at[n], sib_send.at[n, 1], sib_recv.at[n, 1], sibling)
+        return remote(lsend.at[n], lrecv.at[n], sib_send.at[1], sib_recv.at[n % 4, 1], sibling)
 
     def ring(r, kind):
         target = right if kind % 2 == 0 else left
         k = (0, 0, 1, 3, 1, 3)[kind]
         h = (0, 1, 1, 0, 0, 1)[kind]
         if kind < 2:
-            dst, ldst = frecv.at[r, h], flrecv.at[r, h]
+            dst, ldst, sem = frecv.at[r, h], flrecv.at[r, h], f_recv.at[r % 4, h]
         else:
             side = kind % 2
-            dst, ldst = drecv.at[r, side, h], dlrecv.at[r, side, h]
+            dst, ldst, sem = drecv.at[r, side, h], dlrecv.at[r, side, h], d_recv.at[r]
         return (
-            remote(part.at[r, k, h], dst, ring_send.at[r, kind, 0], ring_recv.at[r, kind, 0], target),
-            remote(lpart.at[r, k, h], ldst, ring_send.at[r, kind, 1], ring_recv.at[r, kind, 1], target),
+            remote(part.at[r, k, h], dst, ring_send.at[0], sem.at[0], target),
+            remote(lpart.at[r, k, h], ldst, ring_send.at[1], sem.at[1], target),
         )
 
     def ring_start(r, kind):
@@ -190,30 +211,27 @@
             lpart[r, k, h] = lse
             ring_start(r, kind)
 
-    def out_copy(r):
-        return pltpu.make_async_copy(outbuf.at[r], out_hbm.at[r], out_sem.at[r])
-
     def finish(r):
-        for kind in (2, 3, 4, 5):
-            for copy in ring(r, kind):
-                copy.wait_recv()
+        pltpu.make_async_copy(drecv.at[r], drecv.at[r], d_recv.at[r, 0]).wait()
+        pltpu.make_async_copy(dlrecv.at[r], dlrecv.at[r], d_recv.at[r, 1]).wait()
         for h in range(2):
             (wa, wb, wc), _ = weights(lpart[r, 2, h], dlrecv[r, 0, h], dlrecv[r, 1, h])
-            outbuf[r, :, pl.ds(h * half, half)] = (
+            out_ref[r, :, pl.ds(h * half, half)] = (
                 scaled(wa, part[r, 2, h]) + scaled(wb, drecv[r, 0, h]) + scaled(wc, drecv[r, 1, h])
             ).astype(jnp.bfloat16)
-        out_copy(r).start()
-
-    for r in range(rounds):
-        q_own(r).start()
+
+    for copy in q_load():
+        copy.start()
+    len_copy = pltpu.make_async_copy(len_hbm, len_ref, lensem)
+    len_copy.start()
     for u in range(SLOTS - 1):
         fetch(u // 2, u % 2).start()
     barrier = pltpu.get_barrier_semaphore()
     for neighbour in (left, right, sibling):
         pl.semaphore_signal(barrier, inc=1, device_id={'dcp': neighbour}, device_id_type=pl.DeviceIdType.MESH)
+    q_pack()
+    len_copy.wait()
     pl.semaphore_wait(barrier, 3)
-    for r in range(rounds):
-        q_own(r).wait()
     for r in range(AHEAD):
         q_first(r)
     q_second(0)
@@ -265,21 +283,20 @@
     def _(r):
         finish(r)
 
-    @pl.loop(0, rounds)
-    def _(r):
-        out_copy(r).wait()
-        for kind in range(6):
-            for copy in ring(r, kind):
-                copy.wait_send()
-        q_copy(r, 0, me, right).wait_send()
-        q_copy(r, 1, me, left).wait_send()
-        for kind in range(2, 7):
-            q_copy(r, kind, me, sibling).wait_send()
-
-    @pl.loop(0, steps)
-    def _(n):
-        sib_o(n).wait_send()
-        sib_l(n).wait_send()
+    def sent(ref, sem):
+        pltpu.make_async_copy(ref, ref, sem).wait()
+
+    sent(qbuf.at[:, 0:7], ag_send.at[0])
+    sent(osend, sib_send.at[0])
+    sent(lsend, sib_send.at[1])
+    sent(part.at[:, 0:3], ring_send.at[0])
+    sent(lpart.at[:, 0:3], ring_send.at[1])
+
+
+def put_out(src_ref, dst_ref, sem):
+    copy = pltpu.make_async_copy(src_ref, dst_ref, sem)
+    copy.start()
+    copy.wait()
 
 
 def solution(mesh):
@@ -298,17 +315,19 @@
         cache = jnp.swapaxes(cache_blk, 3, 4).reshape(group, rounds, pages, 1, width, page_len)
         bf16 = jnp.bfloat16
         dma = pltpu.SemaphoreType.DMA
-        return pl.pallas_call(
+        tiles = group * latent // LANES + group // 2
+        hbm = pl.BlockSpec(memory_space=pltpu.HBM)
+        vmem = pl.BlockSpec(memory_space=pltpu.VMEM)
+        out = jax.ShapeDtypeStruct((rounds, heads, latent), bf16)
+        merged = pl.pallas_call(
             functools.partial(kernel, group),
-            out_shape=jax.ShapeDtypeStruct((rounds, heads, latent), bf16),
-            in_specs=[
-                pl.BlockSpec(memory_space=pltpu.SMEM),
-                pl.BlockSpec(memory_space=pl.ANY),
-                pl.BlockSpec(memory_space=pl.ANY),
-            ],
-            out_specs=pl.BlockSpec(memory_space=pl.ANY),
+            out_shape=out,
+            in_specs=[hbm, hbm, hbm],
+            out_specs=vmem,
             scratch_shapes=[
-                pltpu.VMEM((rounds, group, group, own_heads, width), bf16),
+                pltpu.SMEM((batch,), jnp.int32),
+                pltpu.VMEM((group, rounds, own_heads, ROPE_DIM), bf16),
+                pltpu.VMEM((rounds, group, tiles, own_heads, LANES), bf16),
                 pltpu.VMEM((SLOTS, pages, width, page_len), bf16),
                 pltpu.VMEM((steps, heads, latent), bf16),
                 pltpu.VMEM((steps, 1, heads), F32),
@@ -322,20 +341,24 @@
                 pltpu.VMEM((rounds, 2, 1, heads), F32),
                 pltpu.VMEM((rounds, 2, 2, heads, half), F32),
                 pltpu.VMEM((rounds, 2, 2, 1, heads), F32),
-                pltpu.VMEM((rounds, heads, latent), bf16),
+                dma,
                 dma((SLOTS,)),
-                dma((rounds,)),
-                dma((rounds, 7)),
-                dma((rounds, 7)),
-                dma((steps, 2)),
-                dma((steps, 2)),
-                dma((rounds, 6, 2)),
-                dma((rounds, 6, 2)),
-                dma((rounds,)),
+                dma((2,)),
+                dma((1,)),
+                dma((rounds, 3)),
+                dma((2,)),
+                dma((4, 2)),
+                dma((2,)),
+                dma((4, 2, 2)),
+                dma((rounds, 2)),
             ],
             compiler_params=pltpu.CompilerParams(
-                collective_id=0, has_side_effects=True, vmem_limit_bytes=60000 * 1024),
-        )(len_blk, q, cache)
+                collective_id=0, has_side_effects=True, vmem_limit_bytes=VMEM_BYTES),
+        )(*(pltpu.with_memory_space_constraint(x, pltpu.HBM) for x in (len_blk, q, cache)))
+        return pl.pallas_call(
+            put_out, out_shape=out, in_specs=[vmem], out_specs=hbm, scratch_shapes=[dma],
+            compiler_params=pltpu.CompilerParams(vmem_limit_bytes=VMEM_BYTES),
+        )(merged)
 
     return jax.shard_map(
         local_step, mesh=mesh,

time: 125 us -> 114 us (0.912)
  Pallas kernels: 123 us -> 114 us
  local copies, waits for them, and re-layouts: 2.26 us -> 0 us
    pallas_call x1 -> x2, Pallas kernels: 123 us -> 114 us  [the longest x1 113 us: local_step(): pl.pallas_call(functools.partial(kernel, group), out_shape=out, in_specs=...]
    unnamed x1 -> x0, local copies, waits for them, and re-layouts: 2.26 us -> none
where the time goes in v2:
time: 114 us
  Pallas kernels  114 us (100%)
    pallas_call x1, Pallas kernels, local_step(): pl.pallas_call(functools.partial(kernel, group), out_shape=out, in_specs=...  113 us

profile of v2, /device:TPU:112, one launch (start us, length us, event | category | flops | bytes accessed | tf_op | source)
XLA Modules:
  0.0 113.8 jit_solution(2245065843859300205)
XLA Ops:
  0.0 112.8 %shard_map.37.src_ref = bf16[8,128,512]{2,1,0:T(8,128)(2,1)S(1)} custom-call(s32[64]{0:T(128)} %len_hbm.1, bf16[8,8,16,576]{3,2,1,0:T(8,128)(2,1)} %bitcast.4, bf16[8,8,4,1,576,256]{5,4,3,2,1,0:T(8,128)(2,1)} %bitcast.2.c_hbm), custom_call_target="tpu_custom_call" | custom-call | tf_op jit(solution)/shard_map/pallas_call | solution.py:322
  112.8 1.0 shard_map.38

commit v3 on v2

--- a/solution.py
+++ b/solution.py
@@ -28,24 +28,22 @@
     return [columns(one / total) for one in exps], top + jnp.log(total)
 
 
-def scaled(col, block):
-    width = col.shape[1]
-    return jnp.concatenate(
-        [col * block[:, i : i + width] for i in range(0, block.shape[1], width)], axis=1
-    )
-
-
 def kernel(
     group, len_hbm, q_hbm, c_hbm, out_ref,
-    len_ref, rope, qbuf, cbuf, osend, lsend, orecv, lrecv, own, lown, part, lpart, frecv, flrecv, drecv, dlrecv,
+    len_ref, rope, qbuf, cbuf, osend, lsend, orecv, lrecv, own, lown, part, frecv, drecv,
     lensem, csem, qsem, ag_send, ag_recv, sib_send, sib_recv, ring_send, f_recv, d_recv,
 ):
     rounds, _, tiles, own_heads, lanes = qbuf.shape
     chips = group // CORES
     steps = rounds * chips
     seqs = steps * CORES
-    latent = osend.shape[2]
-    half = latent // 2
+    heads, latent = osend.shape[1:]
+    blocks = latent // lanes // 2
+    lse_row = pl.ds(blocks * heads, 1)
+    rows = pl.ds(0, blocks * heads + 1)
+
+    def block_rows(i):
+        return pl.ds(i * heads, heads)
     pages, width, page_len = cbuf.shape[1:]
     me = lax.axis_index('dcp')
     chip, core = me // CORES, me % CORES
@@ -59,6 +57,9 @@
             src_ref=src, dst_ref=dst, send_sem=send, recv_sem=recv,
             device_id={'dcp': target}, device_id_type=pl.DeviceIdType.MESH)
 
+    def wait_bytes(ref, sem):
+        pltpu.make_async_copy(ref, ref, sem).wait()
+
     def place(n, other):
         r, k = n // chips, n % chips
         dest_chip = (chip + 2 - k + chips) % chips
@@ -73,26 +74,22 @@
     latent_tiles = group * latent // lanes
 
     def q_load():
-        yield pltpu.make_async_copy(q_hbm.at[:, :, :, latent:], rope, qsem.at[1])
-        for c in range(latent // lanes):
-            for r in range(rounds):
+        yield pltpu.make_async_copy(q_hbm.at[:, :, :, latent:], rope, qsem.at[2])
+        for r in range(rounds):
+            for c in range(latent // lanes):
                 yield pltpu.make_async_copy(
-                    q_hbm.at[:, r, :, c * lanes : (c + 1) * lanes], qbuf.at[r, me, c * group : (c + 1) * group], qsem.at[0])
-
-    def q_pack():
-        pltpu.make_async_copy(rope, rope, qsem.at[1]).wait()
-        for r in range(rounds):
-            for p in range(group // 2):
-                qbuf[r, me, latent_tiles + p] = jnp.concatenate([rope[2 * p, r], rope[2 * p + 1, r]], axis=1)
-        whole = qbuf.at[:, me, 0:latent_tiles]
-        pltpu.make_async_copy(whole, whole, qsem.at[0]).wait()
+                    q_hbm.at[:, r, :, c * lanes : (c + 1) * lanes], qbuf.at[r, me, c * group : (c + 1) * group],
+                    qsem.at[min(r, 1)])
+
+    def q_pack(r):
+        for p in range(group // 2):
+            qbuf[r, me, latent_tiles + p] = jnp.concatenate([rope[2 * p, r], rope[2 * p + 1, r]], axis=1)
 
     def q_copy(r, kind, block, target):
-        return remote(qbuf.at[r, block], qbuf.at[r, block], ag_send.at[0], ag_recv.at[r, kind], target)
-
-    def q_wait(r, kind, blocks):
-        ref = qbuf.at[r, 0:blocks]
-        pltpu.make_async_copy(ref, ref, ag_recv.at[r, kind]).wait()
+        return remote(qbuf.at[r, block], qbuf.at[r, block], ag_send, ag_recv.at[r, kind], target)
+
+    def q_wait(r, kind, count):
+        wait_bytes(qbuf.at[r, 0:count], ag_recv.at[r, kind])
 
     def q_first(r):
         q_copy(r, 0, me, right).start()
@@ -130,7 +127,6 @@
         def _():
             fetch((2 * n + e + SLOTS - 1) // 2, (e + SLOTS - 1) % 2).start()
 
-        heads = group * own_heads
         q = [qbuf[r, :, c * group + d].reshape(heads, lanes) for c in range(latent // lanes)]
         pair = qbuf[r, :, latent_tiles + d // 2].reshape(heads, lanes)
         q.append(jnp.where(d % 2 == 0, pair[:, : lanes // 2], pair[:, lanes // 2 :]))
@@ -163,18 +159,10 @@
         k = (0, 0, 1, 3, 1, 3)[kind]
         h = (0, 1, 1, 0, 0, 1)[kind]
         if kind < 2:
-            dst, ldst, sem = frecv.at[r, h], flrecv.at[r, h], f_recv.at[r % 4, h]
+            dst, sem = frecv.at[r, h, rows], f_recv.at[r % 4, h]
         else:
-            side = kind % 2
-            dst, ldst, sem = drecv.at[r, side, h], dlrecv.at[r, side, h], d_recv.at[r]
-        return (
-            remote(part.at[r, k, h], dst, ring_send.at[0], sem.at[0], target),
-            remote(lpart.at[r, k, h], ldst, ring_send.at[1], sem.at[1], target),
-        )
-
-    def ring_start(r, kind):
-        for copy in ring(r, kind):
-            copy.start()
+            dst, sem = drecv.at[r, kind % 2, h, rows], d_recv.at[r]
+        return remote(part.at[r, k, h, rows], dst, ring_send, sem, target)
 
     def merge(n):
         r, k = n // chips, n % chips
@@ -183,42 +171,43 @@
         slot = n % 2
         (wa, wb), lse = weights(lown[slot], lrecv[n])
         for h in range(2):
-            cols = pl.ds(h * half, half)
-            part[r, k, h] = scaled(wa, own[slot, :, cols].astype(F32)) + scaled(wb, orecv[n, :, cols].astype(F32))
-            lpart[r, k, h] = lse
+            for i in range(blocks):
+                cols = pl.ds((h * blocks + i) * lanes, lanes)
+                part[r, k, h, block_rows(i)] = wa * own[slot, :, cols].astype(F32) + wb * orecv[n, :, cols].astype(F32)
+            part[r, k, h, lse_row] = lse
 
         @pl.when(k == 0)
         def _():
-            ring_start(r, 0)
-            ring_start(r, 1)
+            ring(r, 0).start()
+            ring(r, 1).start()
 
         @pl.when(k == 1)
         def _():
-            ring_start(r, 2)
+            ring(r, 2).start()
 
         @pl.when(k == 3)
         def _():
-            ring_start(r, 3)
+            ring(r, 3).start()
 
     def relay(r):
         for kind in (4, 5):
             h = kind % 2
             k = (1, 3)[h]
-            for copy in ring(r, h):
-                copy.wait_recv()
-            (wa, wb), lse = weights(lpart[r, k, h], flrecv[r, h])
-            part[r, k, h] = scaled(wa, part[r, k, h]) + scaled(wb, frecv[r, h])
-            lpart[r, k, h] = lse
-            ring_start(r, kind)
+            ring(r, h).wait_recv()
+            (wa, wb), lse = weights(part[r, k, h, lse_row], frecv[r, h, lse_row])
+            for i in range(blocks):
+                part[r, k, h, block_rows(i)] = wa * part[r, k, h, block_rows(i)] + wb * frecv[r, h, block_rows(i)]
+            part[r, k, h, lse_row] = lse
+            ring(r, kind).start()
 
     def finish(r):
-        pltpu.make_async_copy(drecv.at[r], drecv.at[r], d_recv.at[r, 0]).wait()
-        pltpu.make_async_copy(dlrecv.at[r], dlrecv.at[r], d_recv.at[r, 1]).wait()
+        wait_bytes(drecv.at[r, :, :, rows], d_recv.at[r])
         for h in range(2):
-            (wa, wb, wc), _ = weights(lpart[r, 2, h], dlrecv[r, 0, h], dlrecv[r, 1, h])
-            out_ref[r, :, pl.ds(h * half, half)] = (
-                scaled(wa, part[r, 2, h]) + scaled(wb, drecv[r, 0, h]) + scaled(wc, drecv[r, 1, h])
-            ).astype(jnp.bfloat16)
+            parts = [part.at[r, 2, h], drecv.at[r, 0, h], drecv.at[r, 1, h]]
+            cols, _ = weights(*(one[lse_row] for one in parts))
+            for i in range(blocks):
+                total = functools.reduce(jnp.add, [col * one[block_rows(i)] for col, one in zip(cols, parts)])
+                out_ref[r, :, pl.ds((h * blocks + i) * lanes, lanes)] = total.astype(jnp.bfloat16)
 
     for copy in q_load():
         copy.start()
@@ -229,11 +218,17 @@
     barrier = pltpu.get_barrier_semaphore()
     for neighbour in (left, right, sibling):
         pl.semaphore_signal(barrier, inc=1, device_id={'dcp': neighbour}, device_id_type=pl.DeviceIdType.MESH)
-    q_pack()
+    wait_bytes(rope, qsem.at[2])
+    q_pack(0)
+    wait_bytes(qbuf.at[0, me, 0:latent_tiles], qsem.at[0])
+    pl.semaphore_wait(barrier, 3)
+    q_first(0)
+    for r in range(1, rounds):
+        q_pack(r)
+    wait_bytes(qbuf.at[1:rounds, me, 0:latent_tiles], qsem.at[1])
+    for r in range(1, AHEAD):
+        q_first(r)
     len_copy.wait()
-    pl.semaphore_wait(barrier, 3)
-    for r in range(AHEAD):
-        q_first(r)
     q_second(0)
     q_first(AHEAD)
     q_second(1)
@@ -283,14 +278,10 @@
     def _(r):
         finish(r)
 
-    def sent(ref, sem):
-        pltpu.make_async_copy(ref, ref, sem).wait()
-
-    sent(qbuf.at[:, 0:7], ag_send.at[0])
-    sent(osend, sib_send.at[0])
-    sent(lsend, sib_send.at[1])
-    sent(part.at[:, 0:3], ring_send.at[0])
-    sent(lpart.at[:, 0:3], ring_send.at[1])
+    wait_bytes(qbuf.at[:, 0:7], ag_send)
+    wait_bytes(osend, sib_send.at[0])
+    wait_bytes(lsend, sib_send.at[1])
+    wait_bytes(part.at[:, 0:3, :, rows], ring_send)
 
 
 def put_out(src_ref, dst_ref, sem):
@@ -307,10 +298,10 @@
         batch, own_heads, width = q_blk.shape
         pages, page_len = cache_blk.shape[1], cache_blk.shape[3]
         latent = width - ROPE_DIM
-        half = latent // 2
         rounds = batch // group
         heads = own_heads * group
         steps = rounds * chips
+        rows = latent // LANES // 2 * heads + 8
         q = q_blk.reshape(group, rounds, own_heads, width)
         cache = jnp.swapaxes(cache_blk, 3, 4).reshape(group, rounds, pages, 1, width, page_len)
         bf16 = jnp.bfloat16
@@ -335,22 +326,19 @@
                 pltpu.VMEM((steps, 1, heads), F32),
                 pltpu.VMEM((2, heads, latent), bf16),
                 pltpu.VMEM((2, 1, heads), F32),
-                pltpu.VMEM((rounds, chips, 2, heads, half), F32),
-                pltpu.VMEM((rounds, chips, 2, 1, heads), F32),
-                pltpu.VMEM((rounds, 2, heads, half), F32),
-                pltpu.VMEM((rounds, 2, 1, heads), F32),
-                pltpu.VMEM((rounds, 2, 2, heads, half), F32),
-                pltpu.VMEM((rounds, 2, 2, 1, heads), F32),
+                pltpu.VMEM((rounds, chips, 2, rows, LANES), F32),
+                pltpu.VMEM((rounds, 2, rows, LANES), F32),
+                pltpu.VMEM((rounds, 2, 2, rows, LANES), F32),
                 dma,
                 dma((SLOTS,)),
-                dma((2,)),
-                dma((1,)),
+                dma((3,)),
+                dma,
                 dma((rounds, 3)),
                 dma((2,)),
                 dma((4, 2)),
-                dma((2,)),
-                dma((4, 2, 2)),
-                dma((rounds, 2)),
+                dma,
+                dma((4, 2)),
+                dma((rounds,)),
             ],
             compiler_params=pltpu.CompilerParams(
                 collective_id=0, has_side_effects=True, vmem_limit_bytes=VMEM_BYTES),

time: 114 us -> 113 us (level)
  no operation moved by 1% of the time
where the time goes in v3:
time: 113 us
  Pallas kernels  113 us (100%)
    pallas_call x1, Pallas kernels, local_step(): pl.pallas_call(functools.partial(kernel, group), out_shape=out, in_specs=...  112 us

profile of v3, /device:TPU:112, one launch (start us, length us, event | category | flops | bytes accessed | tf_op | source)
XLA Modules:
  0.0 113.0 jit_solution(5249160915571266904)
XLA Ops:
  0.0 112.0 %shard_map.37.src_ref = bf16[8,128,512]{2,1,0:T(8,128)(2,1)S(1)} custom-call(s32[64]{0:T(128)} %len_hbm.1, bf16[8,8,16,576]{3,2,1,0:T(8,128)(2,1)} %bitcast.4, bf16[8,8,4,1,576,256]{5,4,3,2,1,0:T(8,128)(2,1)} %bitcast.2.c_hbm), custom_call_target="tpu_custom_call" | custom-call | tf_op jit(solution)/shard_map/pallas_call | solution.py:313
  112.0 1.0 shard_map.38

commit v4 on v3

--- a/solution.py
+++ b/solution.py
@@ -13,7 +13,7 @@
 SLOTS = 4
 AHEAD = 3
 LANES = 128
-VMEM_BYTES = 46 * 2**20
+VMEM_BYTES = 36 * 2**20
 F32 = jnp.float32
 
 
@@ -28,9 +28,22 @@
     return [columns(one / total) for one in exps], top + jnp.log(total)
 
 
+def finish(local, received, out_ref):
+    heads, latent = out_ref.shape
+    blocks = latent // LANES // 2
+    lse_row = pl.ds(blocks * heads, 1)
+    for h in range(2):
+        parts = [local.at[h], received.at[0, h], received.at[1, h]]
+        cols, _ = weights(*(one[lse_row] for one in parts))
+        for i in range(blocks):
+            rows = pl.ds(i * heads, heads)
+            total = functools.reduce(jnp.add, [col * one[rows] for col, one in zip(cols, parts)])
+            out_ref[:, pl.ds((h * blocks + i) * LANES, LANES)] = total.astype(jnp.bfloat16)
+
+
 def kernel(
-    group, len_hbm, q_hbm, c_hbm, out_ref,
-    len_ref, rope, qbuf, cbuf, osend, lsend, orecv, lrecv, own, lown, part, frecv, drecv,
+    group, len_hbm, q_hbm, c_hbm, out_ref, part, drecv,
+    len_ref, rope, qbuf, cbuf, osend, lsend, orecv, lrecv, own, lown, frecv,
     lensem, csem, qsem, ag_send, ag_recv, sib_send, sib_recv, ring_send, f_recv, d_recv,
 ):
     rounds, _, tiles, own_heads, lanes = qbuf.shape
@@ -74,12 +87,14 @@
     latent_tiles = group * latent // lanes
 
     def q_load():
-        yield pltpu.make_async_copy(q_hbm.at[:, :, :, latent:], rope, qsem.at[2])
+        yield pltpu.make_async_copy(q_hbm.at[:, 0, :, latent:], rope.at[:, 0], qsem.at[2])
         for r in range(rounds):
             for c in range(latent // lanes):
                 yield pltpu.make_async_copy(
                     q_hbm.at[:, r, :, c * lanes : (c + 1) * lanes], qbuf.at[r, me, c * group : (c + 1) * group],
                     qsem.at[min(r, 1)])
+            if r == 0:
+                yield pltpu.make_async_copy(q_hbm.at[:, 1:, :, latent:], rope.at[:, 1:], qsem.at[3])
 
     def q_pack(r):
         for p in range(group // 2):
@@ -200,29 +215,31 @@
             part[r, k, h, lse_row] = lse
             ring(r, kind).start()
 
-    def finish(r):
+    def arrive(r):
         wait_bytes(drecv.at[r, :, :, rows], d_recv.at[r])
-        for h in range(2):
-            parts = [part.at[r, 2, h], drecv.at[r, 0, h], drecv.at[r, 1, h]]
-            cols, _ = weights(*(one[lse_row] for one in parts))
-            for i in range(blocks):
-                total = functools.reduce(jnp.add, [col * one[block_rows(i)] for col, one in zip(cols, parts)])
-                out_ref[r, :, pl.ds((h * blocks + i) * lanes, lanes)] = total.astype(jnp.bfloat16)
-
+
+    barrier = pltpu.get_barrier_semaphore()
+    for neighbour in (left, right, sibling):
+        pl.semaphore_signal(barrier, inc=1, device_id={'dcp': neighbour}, device_id_type=pl.DeviceIdType.MESH)
     for copy in q_load():
         copy.start()
     len_copy = pltpu.make_async_copy(len_hbm, len_ref, lensem)
     len_copy.start()
     for u in range(SLOTS - 1):
         fetch(u // 2, u % 2).start()
-    barrier = pltpu.get_barrier_semaphore()
-    for neighbour in (left, right, sibling):
-        pl.semaphore_signal(barrier, inc=1, device_id={'dcp': neighbour}, device_id_type=pl.DeviceIdType.MESH)
-    wait_bytes(rope, qsem.at[2])
+    pl.semaphore_wait(barrier, 3)
+    for c in range(latent // lanes):
+        to = pl.ds(c * group, group)
+        for target in (right, left):
+            remote(q_hbm.at[:, 0, :, c * lanes : (c + 1) * lanes], qbuf.at[0, me, to], ag_send, ag_recv.at[0, 0], target).start()
+    wait_bytes(rope.at[:, 0], qsem.at[2])
     q_pack(0)
+    to = pl.ds(latent_tiles, group // 2)
+    for target in (right, left):
+        remote(qbuf.at[0, me, to], qbuf.at[0, me, to], ag_send, ag_recv.at[0, 0], target).start()
     wait_bytes(qbuf.at[0, me, 0:latent_tiles], qsem.at[0])
-    pl.semaphore_wait(barrier, 3)
-    q_first(0)
+    q_copy(0, 2, me, sibling).start()
+    wait_bytes(rope.at[:, 1:], qsem.at[3])
     for r in range(1, rounds):
         q_pack(r)
     wait_bytes(qbuf.at[1:rounds, me, 0:latent_tiles], qsem.at[1])
@@ -274,9 +291,12 @@
     merge(steps - 1)
     relay(rounds - 1)
 
-    @pl.loop(0, rounds)
+    @pl.loop(0, rounds - 1)
     def _(r):
-        finish(r)
+        arrive(r)
+        finish(part.at[r, 2], drecv.at[r], out_ref.at[r])
+
+    arrive(rounds - 1)
 
     wait_bytes(qbuf.at[:, 0:7], ag_send)
     wait_bytes(osend, sib_send.at[0])
@@ -284,10 +304,17 @@
     wait_bytes(part.at[:, 0:3, :, rows], ring_send)
 
 
-def put_out(src_ref, dst_ref, sem):
-    copy = pltpu.make_async_copy(src_ref, dst_ref, sem)
-    copy.start()
-    copy.wait()
+def put_out(done, part, drecv, out_hbm, last, sems):
+    n = done.shape[0]
+    copies = [
+        pltpu.make_async_copy(done, out_hbm.at[pl.ds(0, n)], sems.at[0]),
+        pltpu.make_async_copy(last, out_hbm.at[n], sems.at[1]),
+    ]
+    copies[0].start()
+    finish(part.at[n, 2], drecv.at[n], last)
+    copies[1].start()
+    for copy in copies:
+        copy.wait()
 
 
 def solution(mesh):
@@ -309,12 +336,15 @@
         tiles = group * latent // LANES + group // 2
         hbm = pl.BlockSpec(memory_space=pltpu.HBM)
         vmem = pl.BlockSpec(memory_space=pltpu.VMEM)
-        out = jax.ShapeDtypeStruct((rounds, heads, latent), bf16)
-        merged = pl.pallas_call(
+        done, part, drecv = pl.pallas_call(
             functools.partial(kernel, group),
-            out_shape=out,
+            out_shape=[
+                jax.ShapeDtypeStruct((rounds - 1, heads, latent), bf16),
+                jax.ShapeDtypeStruct((rounds, chips, 2, rows, LANES), F32),
+                jax.ShapeDtypeStruct((rounds, 2, 2, rows, LANES), F32),
+            ],
             in_specs=[hbm, hbm, hbm],
-            out_specs=vmem,
+            out_specs=[vmem] * 3,
             scratch_shapes=[
                 pltpu.SMEM((batch,), jnp.int32),
                 pltpu.VMEM((group, rounds, own_heads, ROPE_DIM), bf16),
@@ -326,12 +356,10 @@
                 pltpu.VMEM((steps, 1, heads), F32),
                 pltpu.VMEM((2, heads, latent), bf16),
                 pltpu.VMEM((2, 1, heads), F32),
-                pltpu.VMEM((rounds, chips, 2, rows, LANES), F32),
                 pltpu.VMEM((rounds, 2, rows, LANES), F32),
-                pltpu.VMEM((rounds, 2, 2, rows, LANES), F32),
                 dma,
                 dma((SLOTS,)),
-                dma((3,)),
+                dma((4,)),
                 dma,
                 dma((rounds, 3)),
                 dma((2,)),
@@ -344,9 +372,13 @@
                 collective_id=0, has_side_effects=True, vmem_limit_bytes=VMEM_BYTES),
         )(*(pltpu.with_memory_space_constraint(x, pltpu.HBM) for x in (len_blk, q, cache)))
         return pl.pallas_call(
-            put_out, out_shape=out, in_specs=[vmem], out_specs=hbm, scratch_shapes=[dma],
+            put_out,
+            out_shape=jax.ShapeDtypeStruct((rounds, heads, latent), bf16),
+            in_specs=[vmem] * 3,
+            out_specs=hbm,
+            scratch_shapes=[pltpu.VMEM((heads, latent), bf16), dma((2,))],
             compiler_params=pltpu.CompilerParams(vmem_limit_bytes=VMEM_BYTES),
-        )(merged)
+        )(done, part, drecv)
 
     return jax.shard_map(
         local_step, mesh=mesh,

time: 113 us -> 112 us (level)
  no operation moved by 1% of the time
where the time goes in v4:
time: 112 us
  Pallas kernels  112 us (100%)
    pallas_call x1, Pallas kernels, local_step(): pl.pallas_call(functools.partial(kernel, group), out_shape=[jax.ShapeDtyp...  111 us

profile of v4, /device:TPU:112, one launch (start us, length us, event | category | flops | bytes accessed | tf_op | source)
XLA Modules:
  0.0 112.4 jit_solution(17144496291932727876)
XLA Ops:
  0.0 111.4 %shard_map.37 = (bf16[7,128,512]{2,1,0:T(8,128)(2,1)S(1)}, f32[8,4,2,264,128]{4,3,2,1,0:T(8,128)S(1)}, f32[8,2,2,264,128]{4,3,2,1,0:T(8,128)S(1)}) custom-call(s32[64]{0:T(128)} %len_hbm.1, bf16[8,8,16,576]{3,2,1,0:T(8,128)(2,1)} %bitcast.4, bf16[8,8,4,1,576,256]{5,4,3,2,1,0:T(8,128)(2,1)} %bitcast.2.c_hbm), custom_call_target="tpu_custom_call" | custom-call | tf_op jit(solution)/shard_map/pallas_call | solution.py:339
  111.4 1.0 shard_map.38

commit v5 on v4

--- a/solution.py
+++ b/solution.py
@@ -12,6 +12,7 @@
 CORES = 2
 SLOTS = 4
 AHEAD = 3
+REUSE = 6
 LANES = 128
 VMEM_BYTES = 36 * 2**20
 F32 = jnp.float32
@@ -44,7 +45,7 @@
 def kernel(
     group, len_hbm, q_hbm, c_hbm, out_ref, part, drecv,
     len_ref, rope, qbuf, cbuf, osend, lsend, orecv, lrecv, own, lown, frecv,
-    lensem, csem, qsem, ag_send, ag_recv, sib_send, sib_recv, ring_send, f_recv, d_recv,
+    lensem, csem, qsem, ag_send, ag_recv, sib_q, sib_send, sib_recv, ring_send, f_recv, d_recv,
 ):
     rounds, _, tiles, own_heads, lanes = qbuf.shape
     chips = group // CORES
@@ -100,11 +101,14 @@
         for p in range(group // 2):
             qbuf[r, me, latent_tiles + p] = jnp.concatenate([rope[2 * p, r], rope[2 * p + 1, r]], axis=1)
 
+    def q_sem(r, kind):
+        return sib_q.at[r] if kind == 2 else ag_recv.at[r % REUSE, kind]
+
     def q_copy(r, kind, block, target):
-        return remote(qbuf.at[r, block], qbuf.at[r, block], ag_send, ag_recv.at[r, kind], target)
+        return remote(qbuf.at[r, block], qbuf.at[r, block], ag_send, q_sem(r, kind), target)
 
     def q_wait(r, kind, count):
-        wait_bytes(qbuf.at[r, 0:count], ag_recv.at[r, kind])
+        wait_bytes(qbuf.at[r, 0:count], q_sem(r, kind))
 
     def q_first(r):
         q_copy(r, 0, me, right).start()
@@ -176,7 +180,7 @@
         if kind < 2:
             dst, sem = frecv.at[r, h, rows], f_recv.at[r % 4, h]
         else:
-            dst, sem = drecv.at[r, kind % 2, h, rows], d_recv.at[r]
+            dst, sem = drecv.at[r, kind % 2, h, rows], d_recv.at[(r + 1) // rounds]
         return remote(part.at[r, k, h, rows], dst, ring_send, sem, target)
 
     def merge(n):
@@ -214,9 +218,6 @@
                 part[r, k, h, block_rows(i)] = wa * part[r, k, h, block_rows(i)] + wb * frecv[r, h, block_rows(i)]
             part[r, k, h, lse_row] = lse
             ring(r, kind).start()
-
-    def arrive(r):
-        wait_bytes(drecv.at[r, :, :, rows], d_recv.at[r])
 
     barrier = pltpu.get_barrier_semaphore()
     for neighbour in (left, right, sibling):
@@ -291,12 +292,13 @@
     merge(steps - 1)
     relay(rounds - 1)
 
+    wait_bytes(drecv.at[0 : rounds - 1, :, :, rows], d_recv.at[0])
+
     @pl.loop(0, rounds - 1)
     def _(r):
-        arrive(r)
         finish(part.at[r, 2], drecv.at[r], out_ref.at[r])
 
-    arrive(rounds - 1)
+    wait_bytes(drecv.at[rounds - 1, :, :, rows], d_recv.at[1])
 
     wait_bytes(qbuf.at[:, 0:7], ag_send)
     wait_bytes(osend, sib_send.at[0])
@@ -361,12 +363,13 @@
                 dma((SLOTS,)),
                 dma((4,)),
                 dma,
-                dma((rounds, 3)),
+                dma((REUSE, 2)),
+                dma((rounds,)),
                 dma((2,)),
                 dma((4, 2)),
                 dma,
                 dma((4, 2)),
-                dma((rounds,)),
+                dma((2,)),
             ],
             compiler_params=pltpu.CompilerParams(
                 collective_id=0, has_side_effects=True, vmem_limit_bytes=VMEM_BYTES),

time: 112 us -> 112 us (level)
  no operation moved by 1% of the time
where the time goes in v5:
time: 112 us
  Pallas kernels  112 us (100%)
    pallas_call x1, Pallas kernels, local_step(): pl.pallas_call(functools.partial(kernel, group), out_shape=[jax.ShapeDtyp...  111 us

profile of v5, /device:TPU:112, one launch (start us, length us, event | category | flops | bytes accessed | tf_op | source)
XLA Modules:
  0.0 112.3 jit_solution(11133499753456990128)
XLA Ops:
  0.0 111.3 %shard_map.37 = (bf16[7,128,512]{2,1,0:T(8,128)(2,1)S(1)}, f32[8,4,2,264,128]{4,3,2,1,0:T(8,128)S(1)}, f32[8,2,2,264,128]{4,3,2,1,0:T(8,128)S(1)}) custom-call(s32[64]{0:T(128)} %len_hbm.1, bf16[8,8,16,576]{3,2,1,0:T(8,128)(2,1)} %bitcast.4, bf16[8,8,4,1,576,256]{5,4,3,2,1,0:T(8,128)(2,1)} %bitcast.2.c_hbm), custom_call_target="tpu_custom_call" | custom-call | tf_op jit(solution)/shard_map/pallas_call | solution.py:341
  111.3 1.0 shard_map.38

commit v6 on v5

--- a/solution.py
+++ b/solution.py
@@ -244,13 +244,13 @@
     for r in range(1, rounds):
         q_pack(r)
     wait_bytes(qbuf.at[1:rounds, me, 0:latent_tiles], qsem.at[1])
-    for r in range(1, AHEAD):
-        q_first(r)
+    q_first(1)
     len_copy.wait()
     q_second(0)
-    q_first(AHEAD)
+    q_first(2)
+    q_first(3)
     q_second(1)
-    q_first(AHEAD + 1)
+    q_first(4)
     q_third(0)
 
     @pl.loop(0, rounds)
@@ -263,15 +263,16 @@
         def _():
             q_first(r + AHEAD + 2)
 
-        @pl.when(r + 1 < rounds)
-        def _():
-            q_third(r + 1)
-
         q_last(r)
 
         @pl.loop(0, chips)
         def _(k):
             n = r * chips + k
+
+            @pl.when(jnp.logical_and(k == 2, r + 1 < rounds))
+            def _():
+                q_third(r + 1)
+
             o, lse = attend(n, 0)
             osend[n] = o
             lsend[n] = lse

time: 112 us -> 112 us (level)
  no operation moved by 1% of the time
where the time goes in v6:
time: 112 us
  Pallas kernels  112 us (100%)
    pallas_call x1, Pallas kernels, local_step(): pl.pallas_call(functools.partial(kernel, group), out_shape=[jax.ShapeDtyp...  111 us

profile of v6, /device:TPU:112, one launch (start us, length us, event | category | flops | bytes accessed | tf_op | source)
XLA Modules:
  0.0 112.3 jit_solution(8929858453048133591)
XLA Ops:
  0.0 111.3 %shard_map.37 = (bf16[7,128,512]{2,1,0:T(8,128)(2,1)S(1)}, f32[8,4,2,264,128]{4,3,2,1,0:T(8,128)S(1)}, f32[8,2,2,264,128]{4,3,2,1,0:T(8,128)S(1)}) custom-call(s32[64]{0:T(128)} %len_hbm.1, bf16[8,8,16,576]{3,2,1,0:T(8,128)(2,1)} %bitcast.4, bf16[8,8,4,1,576,256]{5,4,3,2,1,0:T(8,128)(2,1)} %bitcast.2.c_hbm), custom_call_target="tpu_custom_call" | custom-call | tf_op jit(solution)/shard_map/pallas_call | solution.py:342
  111.3 1.0 shard_map.38

commit v7 on v6

--- a/solution.py
+++ b/solution.py
@@ -10,7 +10,7 @@
 ROPE_DIM = 64
 QK_DIM = 192
 CORES = 2
-SLOTS = 4
+SLOTS = 3
 AHEAD = 3
 REUSE = 6
 LANES = 128
@@ -102,7 +102,7 @@
             qbuf[r, me, latent_tiles + p] = jnp.concatenate([rope[2 * p, r], rope[2 * p + 1, r]], axis=1)
 
     def q_sem(r, kind):
-        return sib_q.at[r] if kind == 2 else ag_recv.at[r % REUSE, kind]
+        return sib_q.at[r % REUSE] if kind == 2 else ag_recv.at[r % REUSE, kind]
 
     def q_copy(r, kind, block, target):
         return remote(qbuf.at[r, block], qbuf.at[r, block], ag_send, q_sem(r, kind), target)
@@ -178,7 +178,7 @@
         k = (0, 0, 1, 3, 1, 3)[kind]
         h = (0, 1, 1, 0, 0, 1)[kind]
         if kind < 2:
-            dst, sem = frecv.at[r, h, rows], f_recv.at[r % 4, h]
+            dst, sem = frecv.at[r, h, rows], f_recv.at[r % 4]
         else:
             dst, sem = drecv.at[r, kind % 2, h, rows], d_recv.at[(r + 1) // rounds]
         return remote(part.at[r, k, h, rows], dst, ring_send, sem, target)
@@ -209,10 +209,10 @@
             ring(r, 3).start()
 
     def relay(r):
+        wait_bytes(frecv.at[r, :, rows], f_recv.at[r % 4])
         for kind in (4, 5):
             h = kind % 2
             k = (1, 3)[h]
-            ring(r, h).wait_recv()
             (wa, wb), lse = weights(part[r, k, h, lse_row], frecv[r, h, lse_row])
             for i in range(blocks):
                 part[r, k, h, block_rows(i)] = wa * part[r, k, h, block_rows(i)] + wb * frecv[r, h, block_rows(i)]
@@ -365,11 +365,11 @@
                 dma((4,)),
                 dma,
                 dma((REUSE, 2)),
-                dma((rounds,)),
+                dma((REUSE,)),
                 dma((2,)),
                 dma((4, 2)),
                 dma,
-                dma((4, 2)),
+                dma((4,)),
                 dma((2,)),
             ],
             compiler_params=pltpu.CompilerParams(

time: 112 us -> 112 us (level)
  no operation moved by 1% of the time
where the time goes in v7:
time: 112 us
  Pallas kernels  112 us (100%)
    pallas_call x1, Pallas kernels, local_step(): pl.pallas_call(functools.partial(kernel, group), out_shape=[jax.ShapeDtyp...  111 us

profile of v7, /device:TPU:112, one launch (start us, length us, event | category | flops | bytes accessed | tf_op | source)
XLA Modules:
  0.0 112.2 jit_solution(5572922390822819948)
XLA Ops:
  0.0 111.2 %shard_map.37 = (bf16[7,128,512]{2,1,0:T(8,128)(2,1)S(1)}, f32[8,4,2,264,128]{4,3,2,1,0:T(8,128)S(1)}, f32[8,2,2,264,128]{4,3,2,1,0:T(8,128)S(1)}) custom-call(s32[64]{0:T(128)} %len_hbm.1, bf16[8,8,16,576]{3,2,1,0:T(8,128)(2,1)} %bitcast.4, bf16[8,8,4,1,576,256]{5,4,3,2,1,0:T(8,128)(2,1)} %bitcast.2.c_hbm), custom_call_target="tpu_custom_call" | custom-call | tf_op jit(solution)/shard_map/pallas_call | solution.py:342
  111.2 1.0 shard_map.38

commit v8 on v7

--- a/solution.py
+++ b/solution.py
@@ -299,12 +299,11 @@
     def _(r):
         finish(part.at[r, 2], drecv.at[r], out_ref.at[r])
 
-    wait_bytes(drecv.at[rounds - 1, :, :, rows], d_recv.at[1])
-
     wait_bytes(qbuf.at[:, 0:7], ag_send)
     wait_bytes(osend, sib_send.at[0])
     wait_bytes(lsend, sib_send.at[1])
     wait_bytes(part.at[:, 0:3, :, rows], ring_send)
+    wait_bytes(drecv.at[rounds - 1, :, :, rows], d_recv.at[1])
 
 
 def put_out(done, part, drecv, out_hbm, last, sems):

time: 112 us -> 112 us (level)
  no operation moved by 1% of the time
where the time goes in v8:
time: 112 us
  Pallas kernels  112 us (100%)
    pallas_call x1, Pallas kernels, local_step(): pl.pallas_call(functools.partial(kernel, group), out_shape=[jax.ShapeDtyp...  111 us

profile of v8, /device:TPU:112, one launch (start us, length us, event | category | flops | bytes accessed | tf_op | source)
XLA Modules:
  0.0 112.2 jit_solution(7878380465675653619)
XLA Ops:
  0.0 111.2 %shard_map.37 = (bf16[7,128,512]{2,1,0:T(8,128)(2,1)S(1)}, f32[8,4,2,264,128]{4,3,2,1,0:T(8,128)S(1)}, f32[8,2,2,264,128]{4,3,2,1,0:T(8,128)S(1)}) custom-call(s32[64]{0:T(128)} %len_hbm.1, bf16[8,8,16,576]{3,2,1,0:T(8,128)(2,1)} %bitcast.4, bf16[8,8,4,1,576,256]{5,4,3,2,1,0:T(8,128)(2,1)} %bitcast.2.c_hbm), custom_call_target="tpu_custom_call" | custom-call | tf_op jit(solution)/shard_map/pallas_call | solution.py:341
  111.2 1.0 shard_map.38

commit v9 on v8

--- a/solution.py
+++ b/solution.py
@@ -45,7 +45,7 @@
 def kernel(
     group, len_hbm, q_hbm, c_hbm, out_ref, part, drecv,
     len_ref, rope, qbuf, cbuf, osend, lsend, orecv, lrecv, own, lown, frecv,
-    lensem, csem, qsem, ag_send, ag_recv, sib_q, sib_send, sib_recv, ring_send, f_recv, d_recv,
+    csem, qsem, ag_send, ag_recv, sib_q, sib_send, sib_recv, ring_send, f_recv, d_recv,
 ):
     rounds, _, tiles, own_heads, lanes = qbuf.shape
     chips = group // CORES
@@ -224,8 +224,6 @@
         pl.semaphore_signal(barrier, inc=1, device_id={'dcp': neighbour}, device_id_type=pl.DeviceIdType.MESH)
     for copy in q_load():
         copy.start()
-    len_copy = pltpu.make_async_copy(len_hbm, len_ref, lensem)
-    len_copy.start()
     for u in range(SLOTS - 1):
         fetch(u // 2, u % 2).start()
     pl.semaphore_wait(barrier, 3)
@@ -239,6 +237,8 @@
     for target in (right, left):
         remote(qbuf.at[0, me, to], qbuf.at[0, me, to], ag_send, ag_recv.at[0, 0], target).start()
     wait_bytes(qbuf.at[0, me, 0:latent_tiles], qsem.at[0])
+    len_copy = pltpu.make_async_copy(len_hbm, len_ref, qsem.at[0])
+    len_copy.start()
     q_copy(0, 2, me, sibling).start()
     wait_bytes(rope.at[:, 1:], qsem.at[3])
     for r in range(1, rounds):
@@ -359,7 +359,6 @@
                 pltpu.VMEM((2, heads, latent), bf16),
                 pltpu.VMEM((2, 1, heads), F32),
                 pltpu.VMEM((rounds, 2, rows, LANES), F32),
-                dma,
                 dma((SLOTS,)),
                 dma((4,)),
                 dma,

time: 112 us -> 112 us (level)
  no operation moved by 1% of the time
where the time goes in v9:
time: 112 us
  Pallas kernels  112 us (100%)
    pallas_call x1, Pallas kernels, local_step(): pl.pallas_call(functools.partial(kernel, group), out_shape=[jax.ShapeDtyp...  111 us

profile of v9, /device:TPU:112, one launch (start us, length us, event | category | flops | bytes accessed | tf_op | source)
XLA Modules:
  0.0 112.2 jit_solution(5771374934917684919)
XLA Ops:
  0.0 111.2 %shard_map.37 = (bf16[7,128,512]{2,1,0:T(8,128)(2,1)S(1)}, f32[8,4,2,264,128]{4,3,2,1,0:T(8,128)S(1)}, f32[8,2,2,264,128]{4,3,2,1,0:T(8,128)S(1)}) custom-call(s32[64]{0:T(128)} %len_hbm.1, bf16[8,8,16,576]{3,2,1,0:T(8,128)(2,1)} %bitcast.4, bf16[8,8,4,1,576,256]{5,4,3,2,1,0:T(8,128)(2,1)} %bitcast.2.c_hbm), custom_call_target="tpu_custom_call" | custom-call | tf_op jit(solution)/shard_map/pallas_call | solution.py:341
  111.2 1.0 shard_map.38
